TPU v7x, 512 devices: a whole 4x8x8 slice. The times are simulated.
512 devices in a mesh: row: 16 (over x_hi, z), col: 32 (over y, x_lo, core).
Axes of the slice: x: 4 (x_hi: 2, x_lo: 2; x = x_hi * 2 + x_lo), y: 8, z: 8, core: 2. Of those that a mesh axis runs over, the one named last changes fastest.
Arguments:
- raw_records: bfloat16 [2048, 768], P(('row', 'col')), may hold values from -6 to 6
- filter_taps: float32 [129], replicated, may hold values from -0.5 to 0.5
- lag_picks: int32 [2048, 2048], P('row', 'col'), may hold values from -2 to 2
- pair_valid: int32 [2048, 2048], P('row', 'col'), may hold values 0 or 1
- clock_offset: float32 [2048], P(('row', 'col')), may hold values from -12 to 12
- clock_drift: float32 [2048], P(('row', 'col')), may hold values from -3 to 3
- var_offset: float32 [2048], P(('row', 'col')), may hold values from 0.5 to 2
- cov_cross: float32 [2048], P(('row', 'col')), may hold values from -0.4 to 0.4
- var_drift: float32 [2048], P(('row', 'col')), may hold values from 0.5 to 2
Outputs:
- pair_misfit: float32 [2048, 2048], P('row', 'col')
- new_offset: float32 [2048], P(('row', 'col'))
- new_drift: float32 [2048], P(('row', 'col'))
- new_var_offset: float32 [2048], P(('row', 'col'))
- new_cov_cross: float32 [2048], P(('row', 'col'))
- new_var_drift: float32 [2048], P(('row', 'col'))
All inputs are finite; a program needn't handle non-finite values. No bound on the sum of `pair_valid` on one device may be relied on, other than what follows from the above.
Results may differ from a plain program's by a relative error of at most 0.0008.
Values may be sent and summed in bfloat16 or wider, within the bound.
No kernel may reach another device: no remote copies, remote signals or barrier semaphores. Data moves between devices by JAX's collectives and lax.ppermute only.
A program may use at most 64 MiB of HBM per device.

v0:
```python
import math
import jax
import jax.numpy as jnp
from jax import lax
from jax.sharding import PartitionSpec as P

LAG = 2
EPS = 1e-06
RHO = 0.5
Q_OFFSET = 0.05
Q_DRIFT = 0.01


def whiten(raw_rows, filter_taps):
    signal = raw_rows.astype(jnp.float32)[:, None, :]
    kernel = filter_taps[None, None, :]
    filtered = lax.conv_general_dilated(
        signal,
        kernel,
        (1,),
        "VALID",
        dimension_numbers=("NCH", "OIH", "NCH"),
        precision=lax.Precision.HIGHEST,
    )[:, 0, :]
    scaling = jnp.sqrt(jnp.mean(filtered * filtered, axis=1, keepdims=True) + EPS)
    return (filtered / scaling).astype(jnp.bfloat16)


def fitted_lag(white_rows, column_white, pick_rows):
    window = white_rows.shape[1] - 128
    centre_rows = white_rows[:, 64 : 64 + window]
    before_lag = jnp.zeros(pick_rows.shape, jnp.float32)
    at_lag = jnp.zeros(pick_rows.shape, jnp.float32)
    after_lag = jnp.zeros(pick_rows.shape, jnp.float32)
    for shift in range(-LAG - 1, LAG + 2):
        shifted = column_white[:, 64 + shift : 64 + shift + window]
        correl = lax.dot_general(
            centre_rows, shifted, (((1,), (1,)), ((), ())), preferred_element_type=jnp.float32
        ) / math.sqrt(window)
        before_lag = before_lag + jnp.where(pick_rows - 1 == shift, correl, 0.0)
        at_lag = at_lag + jnp.where(pick_rows == shift, correl, 0.0)
        after_lag = after_lag + jnp.where(pick_rows + 1 == shift, correl, 0.0)
    spread = jnp.maximum(
        jnp.sqrt(before_lag * before_lag + at_lag * at_lag + after_lag * after_lag), 1.0
    )
    return pick_rows.astype(jnp.float32) + (after_lag - before_lag) / spread


def local(
    raw_records,
    filter_taps,
    lag_picks,
    pair_valid,
    clock_offset,
    clock_drift,
    var_offset,
    cov_cross,
    var_drift,
):
    per_device = raw_records.shape[0]
    rows_count = lax.axis_size("row")
    cols_count = lax.axis_size("col")
    stations = per_device * rows_count * cols_count
    offset_pred = clock_offset + clock_drift
    voff = var_offset + 2.0 * cov_cross + var_drift + Q_OFFSET
    vcross = cov_cross + var_drift
    vdrift = var_drift + Q_DRIFT
    everyone = lax.all_gather(offset_pred, ("row", "col"), axis=0, tiled=True)
    offset_grid = everyone.reshape(rows_count, cols_count, per_device)
    row_index = lax.axis_index("row")
    col_index = lax.axis_index("col")
    row_offsets = lax.dynamic_index_in_dim(offset_grid, row_index, 0, keepdims=False).reshape(-1)
    column_offsets = lax.dynamic_index_in_dim(offset_grid, col_index, 1, keepdims=False).reshape(-1)
    valid_float = pair_valid.astype(jnp.float32)
    own_white = whiten(raw_records, filter_taps)
    column_white = lax.all_gather(own_white, "row", axis=0, tiled=True)
    white_rows = lax.all_gather(own_white, "col", axis=0, tiled=True)
    count = white_rows.shape[0]
    pick_rows = lax.slice_in_dim(lag_picks, 0, count, axis=0)
    valid_rows = lax.slice_in_dim(valid_float, 0, count, axis=0)
    offset_rows = lax.slice_in_dim(row_offsets, 0, count, axis=0)
    lagged = fitted_lag(white_rows, column_white, pick_rows)
    pair_misfit = valid_rows * (lagged - offset_rows[:, None] + column_offsets[None, :])
    row_terms = (jnp.sum(pair_misfit, axis=1), jnp.sum(valid_float, axis=1))
    column_terms = (-jnp.sum(pair_misfit, axis=0), jnp.sum(valid_float, axis=0))
    row_whole = lax.psum((row_terms[0], row_terms[1]), "col")
    column_whole = lax.psum((column_terms[0], column_terms[1]), "row")
    row_misfit = lax.dynamic_slice_in_dim(row_whole[0], col_index * per_device, per_device, 0)
    row_pairs = lax.dynamic_slice_in_dim(row_whole[1], col_index * per_device, per_device, 0)
    column_misfit = lax.dynamic_slice_in_dim(column_whole[0], row_index * per_device, per_device, 0)
    column_pairs = lax.dynamic_slice_in_dim(column_whole[1], row_index * per_device, per_device, 0)
    innovation = row_misfit + column_misfit
    pairs = row_pairs + column_pairs
    denom = pairs * voff + RHO * stations
    share = innovation / denom
    new_offset = offset_pred + voff * share
    new_drift = clock_drift + vcross * share
    new_var_offset = voff - voff * voff * pairs / denom
    new_cov_cross = vcross - voff * vcross * pairs / denom
    new_var_drift = vdrift - vcross * vcross * pairs / denom
    return (pair_misfit, new_offset, new_drift, new_var_offset, new_cov_cross, new_var_drift)


def solution(mesh):
    in_specs = (
        P(("row", "col"), None),
        P(),
        P("row", "col"),
        P("row", "col"),
        P(("row", "col")),
        P(("row", "col")),
        P(("row", "col")),
        P(("row", "col")),
        P(("row", "col")),
    )
    out_specs = (
        P("row", "col"),
        P(("row", "col")),
        P(("row", "col")),
        P(("row", "col")),
        P(("row", "col")),
        P(("row", "col")),
    )
    return jax.shard_map(local, mesh=mesh, in_specs=in_specs, out_specs=out_specs, check_vma=False)
```

profile of v0, /device:TPU:1, one launch (start us, length us, event | category | flops | bytes accessed | tf_op | source)
XLA Modules:
  0.0 324.8 jit_solution(12213304597258253916)
XLA Ops:
  0.7 0.6 copy-done.2
  1.4 106.1 %all-reduce = f32[2048]{0:T(1024)S(1)} all-reduce(f32[2048]{0:T(1024)S(1)} %get-tuple-element.19), channel_id=1, replica_groups=mesh['row'=16,'col'=32] {'row','col'}, use_global_device_ids=true, to_apply=%add | all-reduce | flops 2048 | bytes 16384
  107.5 0.3 reshape.27
  108.0 0.6 copy-done.1
  108.6 0.4 copy.20
  109.0 0.7 copy-done.5
  109.7 0.1 copy.21
  109.8 49.0 %fusion.21 = f32[4,1,640]{0,1,2:T(1,128)S(1)} fusion(bf16[4,1,768]{0,1,2:T(2,128)(2,1)S(1)} %copy.20, f32[1,1,129]{1,0,2:T(1,128)S(1)} %copy.21), kind=kOutput, calls=%fused_computation.51 | convolution fusion | flops 3962880 | bytes 16900 | tf_op jit(solution)/shard_map/conv_general_dilated | solution.py:17
  159.1 33.0 %all-gather = bf16[32,4,640]{2,1,0:T(4,128)(2,1)S(1)} all-gather(bf16[1,4,640]{2,1,0:T(4,128)(2,1)S(1)} %copy.22), channel_id=1, replica_groups=mesh['row'=16,'col'=32] {'col'}, dimensions={0}, use_global_device_ids=true | all-gather | bytes 168960 | tf_op jit(solution)/shard_map/all_gather | solution.py:77
  192.1 30.2 %all-gather.1 = bf16[16,4,640]{2,1,0:T(4,128)(2,1)S(1)} all-gather(bf16[1,4,640]{2,1,0:T(4,128)(2,1)S(1)} %copy.22), channel_id=1, replica_groups=mesh['row'=16,'col'=32] {'row'}, dimensions={0}, use_global_device_ids=true | all-gather | bytes 87040 | tf_op jit(solution)/shard_map/all_gather | solution.py:76
  222.3 0.2 convolution_multiply_fusion.6
  222.6 0.3 convolution_multiply_fusion.5
  222.8 0.3 convolution_multiply_fusion.4
  223.1 0.3 convolution_multiply_fusion.3
  223.3 0.3 convolution_multiply_fusion.2
  223.6 0.2 convolution_multiply_fusion.1
  223.8 0.5 copy-done
  224.4 1.0 fusion.19
  225.5 30.2 %all-reduce.2 = (f32[64]{0:T(128)S(1)}, f32[64]{0:T(128)S(1)}) all-reduce(f32[64]{0:T(128)S(1)} %neg.3, f32[64]{0:T(128)S(1)} %get-tuple-element.7), channel_id=1, replica_groups=mesh['row'=16,'col'=32] {'row'}, use_global_device_ids=true, to_apply=%region_4.5 | all-reduce | flops 128 | bytes 1024 | tf_op jit(solution)/shard_map/psum | solution.py:87
  255.7 66.7 %all-reduce.1 = (f32[128]{0:T(128)S(1)}, f32[128]{0:T(128)S(1)}) all-reduce(f32[128]{0:T(128)S(1)} %get-tuple-element.8, f32[128]{0:T(128)S(1)} %get-tuple-element.6), channel_id=1, replica_groups=mesh['row'=16,'col'=32] {'col'}, use_global_device_ids=true, to_apply=%region_2.3 | all-reduce | flops 256 | bytes 2048 | tf_op jit(solution)/shard_map/psum | solution.py:86
  322.4 0.6 copy-done.3
  323.1 0.6 divide_subtract_fusion
  323.7 0.6 multiply_add_fusion
  324.3 0.5 multiply_add_fusion.1
  (27 shorter events, 0.9 us)
Async XLA Ops:
  0.6 0.7 copy-start.2
  0.7 0.7 copy-start.6
  107.9 0.7 copy-start.1
  109.0 0.7 copy-start.5
  223.6 0.8 copy-start
  223.6 0.8 copy-start.8
  322.4 0.7 copy-start.3
  322.4 0.7 copy-start.4
  322.4 0.7 copy-start.7
where the time goes:
time: 325 us
  blocking collectives  266 us (82%)
  matrix products  51.5 us (16%)
  local copies, waits for them, and re-layouts  4.3 us (1%)
    unnamed x1, blocking collectives  106 us
    psum x1, blocking collectives, local(): row_whole = lax.psum((row_terms[0], row_terms[1]), 'col')  66.7 us
    conv_general_dilated x1, matrix products, whiten(): lax.conv_general_dilated(signal, kernel, (1,), 'VALID', dimension_numbers...  49 us
    all_gather x1, blocking collectives, local(): white_rows = lax.all_gather(own_white, 'col', axis=0, tiled=True)  33 us
    all_gather x1, blocking collectives, local(): column_white = lax.all_gather(own_white, 'row', axis=0, tiled=True)  30.2 us
    psum x1, blocking collectives, local(): column_whole = lax.psum((column_terms[0], column_terms[1]), 'row')  30.2 us

commit v1 on v0

--- a/solution.py
+++ b/solution.py
@@ -73,7 +73,9 @@
     column_offsets = lax.dynamic_index_in_dim(offset_grid, col_index, 1, keepdims=False).reshape(-1)
     valid_float = pair_valid.astype(jnp.float32)
     own_white = whiten(raw_records, filter_taps)
-    column_white = lax.all_gather(own_white, "row", axis=0, tiled=True)
+    column_white = jnp.concatenate(
+        lax.all_to_all(jnp.stack([own_white] * lax.axis_size("row")), "row", 0, 0), axis=0
+    )
     white_rows = lax.all_gather(own_white, "col", axis=0, tiled=True)
     count = white_rows.shape[0]
     pick_rows = lax.slice_in_dim(lag_picks, 0, count, axis=0)

time: 325 us -> 298 us (0.917)
  blocking collectives: 266 us -> 224 us
  starting transfers between devices: 0 us -> 13.4 us
    all_gather x1 -> x0, blocking collectives: 30.2 us -> none  [local(): column_white = lax.all_gather(own_white, 'row', axis=0, tiled=True)]
    all_to_all x0 -> x1, starting transfers between devices: none -> 13.4 us  [local(): lax.all_to_all(jnp.stack([own_white] * lax.axis_size('row')), 'row', 0, 0)]
    unnamed x1, blocking collectives: 106 us -> 99 us
    psum x1, blocking collectives: 66.7 us -> 59.7 us  [local(): row_whole = lax.psum((row_terms[0], row_terms[1]), 'col')]
  transfers between devices with their start and end apart: 0 -> 1, of which waited for: 0 -> 0; matrix products, arithmetic and copies ran while one was open for 0% -> 0% of each run, Pallas kernels for 0% -> 0%
where the time goes in v1:
time: 298 us; the launch traced here: 297 us
  blocking collectives  224 us (75%)
  matrix products  51.5 us (17%)
  starting transfers between devices  13.4 us (4%)
  local copies, waits for them, and re-layouts  5.69 us (2%)
    unnamed x1, blocking collectives  99 us
    psum x1, blocking collectives, local(): row_whole = lax.psum((row_terms[0], row_terms[1]), 'col')  59.7 us
    conv_general_dilated x1, matrix products, whiten(): lax.conv_general_dilated(signal, kernel, (1,), 'VALID', dimension_numbers...  49 us
    all_gather x1, blocking collectives, local(): white_rows = lax.all_gather(own_white, 'col', axis=0, tiled=True)  33.1 us
    psum x1, blocking collectives, local(): column_whole = lax.psum((column_terms[0], column_terms[1]), 'row')  31.8 us
    all_to_all x1, starting transfers between devices, local(): lax.all_to_all(jnp.stack([own_white] * lax.axis_size('row')), 'row', 0, 0)  13.4 us
  transfers between devices with their start and end apart: 1, of which 0 were waited for; matrix products, arithmetic and copies ran while one was open for 0% of the time, Pallas kernels for 0%

profile of v1, /device:TPU:1, one launch (start us, length us, event | category | flops | bytes accessed | tf_op | source)
XLA Modules:
  0.0 297.1 jit_solution(11659150843311396388)
XLA Ops:
  0.6 1.1 copy.21
  1.7 0.7 copy-done.4
  2.5 49.0 %fusion.20 = f32[4,1,640]{0,1,2:T(1,128)S(1)} fusion(bf16[4,1,768]{0,1,2:T(2,128)(2,1)S(1)} %copy.21, f32[1,1,129]{1,0,2:T(1,128)S(1)} %copy.22), kind=kOutput, calls=%fused_computation.50 | convolution fusion | flops 3962880 | bytes 16900 | tf_op jit(solution)/shard_map/conv_general_dilated | solution.py:17
  51.8 0.7 stack.2
  52.4 13.4 %all-to-all-start = ((bf16[16,4,640]{2,1,0:T(4,128)(2,1)}), bf16[16,4,640]{2,1,0:T(4,128)(2,1)S(1)}, u32[]{:S(2)}, u32[]{:S(2)}) async-start(bf16[16,4,640]{2,1,0:T(4,128)(2,1)} %stack.2), calls=%async_computation | async-start | bytes 163840 | tf_op jit(solution)/shard_map/all_to_all | solution.py:77
  66.1 0.6 copy-done.1
  66.8 99.0 %all-reduce = f32[2048]{0:T(1024)S(1)} all-reduce(f32[2048]{0:T(1024)S(1)} %get-tuple-element.19), channel_id=1, replica_groups=mesh['row'=16,'col'=32] {'row','col'}, use_global_device_ids=true, to_apply=%add | all-reduce | flops 2048 | bytes 16384
  165.9 0.3 reshape.40
  166.1 33.1 %all-gather = bf16[32,4,640]{2,1,0:T(4,128)(2,1)S(1)} all-gather(bf16[1,4,640]{2,1,0:T(4,128)(2,1)S(1)} %copy.23), channel_id=1, replica_groups=mesh['row'=16,'col'=32] {'col'}, dimensions={0}, use_global_device_ids=true | all-gather | bytes 168960 | tf_op jit(solution)/shard_map/all_gather | solution.py:79
  199.5 0.5 copy-done
  200.1 0.2 convolution_multiply_fusion.6
  200.4 0.3 convolution_multiply_fusion.5
  200.6 0.3 convolution_multiply_fusion.4
  200.9 0.3 convolution_multiply_fusion.3
  201.1 0.3 convolution_multiply_fusion.2
  201.4 0.2 convolution_multiply_fusion.1
  201.7 0.5 copy-done.7
  202.2 1.0 fusion.18
  203.2 31.8 %all-reduce.2 = (f32[64]{0:T(128)S(1)}, f32[64]{0:T(128)S(1)}) all-reduce(f32[64]{0:T(128)S(1)} %neg.3, f32[64]{0:T(128)S(1)} %get-tuple-element.7), channel_id=1, replica_groups=mesh['row'=16,'col'=32] {'row'}, use_global_device_ids=true, to_apply=%region_4.5 | all-reduce | flops 128 | bytes 1024 | tf_op jit(solution)/shard_map/psum | solution.py:89
  235.0 59.7 %all-reduce.1 = (f32[128]{0:T(128)S(1)}, f32[128]{0:T(128)S(1)}) all-reduce(f32[128]{0:T(128)S(1)} %get-tuple-element.8, f32[128]{0:T(128)S(1)} %get-tuple-element.6), channel_id=1, replica_groups=mesh['row'=16,'col'=32] {'col'}, use_global_device_ids=true, to_apply=%region_2.3 | all-reduce | flops 256 | bytes 2048 | tf_op jit(solution)/shard_map/psum | solution.py:88
  294.8 0.6 copy-done.2
  295.4 0.6 divide_subtract_fusion
  296.0 0.6 multiply_add_fusion
  296.6 0.5 multiply_add_fusion.1
  (29 shorter events, 1.1 us)
Async XLA Ops:
  1.7 0.7 copy-start.4
  52.4 147.7 %all-to-all-start = ((bf16[16,4,640]{2,1,0:T(4,128)(2,1)}), bf16[16,4,640]{2,1,0:T(4,128)(2,1)S(1)}, u32[]{:S(2)}, u32[]{:S(2)}) async-start(bf16[16,4,640]{2,1,0:T(4,128)(2,1)} %stack.2), calls=%async_computation | async-start | bytes 163840 | tf_op jit(solution)/shard_map/all_to_all | solution.py:77
  66.0 0.7 copy-start.1
  66.1 0.7 copy-start.5
  199.2 0.8 copy-start
  201.4 0.8 copy-start.7
  294.8 0.7 copy-start.2
  294.8 0.7 copy-start.3
  294.8 0.7 copy-start.6
